TPU v7x, 32 devices: a whole 2x2x4 slice. The times are simulated.
32 devices in a mesh: dp: 8 (over z, x), expert: 4 (over y, core).
Axes of the slice: x: 2, y: 2, z: 4, core: 2. Of those that a mesh axis runs over, the one named last changes fastest.
Arguments:
- tokens: bfloat16 [4096, 4096], P(('dp', 'expert')), may hold values from -6 to 6
- select: int32 [4, 128], P(None, ('dp', 'expert')), may hold values from -1 to 127, as said below
- gates: float32 [4, 128], P(None, ('dp', 'expert')), may hold values from 0.1 to 1
- w_gate: bfloat16 [4, 4096, 8192], P('expert', None, 'dp'), may hold values from -0.09375 to 0.09375
- w_up: bfloat16 [4, 4096, 8192], P('expert', None, 'dp'), may hold values from -0.09375 to 0.09375
- w_down: bfloat16 [4, 8192, 4096], P('expert', 'dp'), may hold values from -0.0625 to 0.0625
Outputs:
- mixed: bfloat16 [4096, 4096], P(('dp', 'expert'))
Inputs may be any that keep to these rules, and one draw needn't show every extreme that they name: `select`: in each block of 4 slots of a row, the live entries come first, distinct and ascending, below 128, followed by -1; every block holds at least one live entry, and every expert fills all 4 slots of some source device.
All inputs are finite; a program needn't handle non-finite values.
Results may differ from a plain program's by a relative error of at most 0.0085.
Values may be sent and summed in bfloat16 or wider, within the bound.
No kernel may reach another device: no remote copies, remote signals or barrier semaphores. Data moves between devices by JAX's collectives and lax.ppermute only.
A program may use at most 64 MiB of HBM per device.

v0:
```python
import jax
import jax.numpy as jnp
from jax import lax
from jax.sharding import PartitionSpec as P


def expert_ffn(block_rows, w_gate, w_up, w_down):
    gate_val = jnp.einsum("erd,edf->erf", block_rows, w_gate, preferred_element_type=jnp.float32)
    up_val = jnp.einsum("erd,edf->erf", block_rows, w_up, preferred_element_type=jnp.float32)
    hidden = (jax.nn.silu(gate_val) * up_val).astype(jnp.bfloat16)
    return jnp.einsum("erf,efd->erd", hidden, w_down, preferred_element_type=jnp.float32)


def per_device(tokens, select, gates, w_gate, w_up, w_down):
    experts, slot_count = select.shape
    tok_dev, width = tokens.shape
    is_live = select >= 0
    safe_idx = jnp.where(is_live, select, 0)
    sel_rows = jnp.take(tokens, safe_idx.reshape(-1), axis=0).reshape(experts, slot_count, width)
    sel_rows = jnp.where(is_live[:, :, None], sel_rows, 0)
    arrived = lax.all_to_all(sel_rows, "expert", split_axis=0, concat_axis=1, tiled=True)
    partial_value = expert_ffn(
        lax.all_gather(arrived, "dp", axis=1, tiled=True), w_gate, w_up, w_down
    )
    summed = lax.psum_scatter(partial_value, "dp", scatter_dimension=1, tiled=True)
    returned = lax.all_to_all(
        summed.astype(jnp.bfloat16), "expert", split_axis=1, concat_axis=0, tiled=True
    )
    weight_flat = jnp.where(is_live, gates, 0.0).reshape(-1)
    token_ids = jnp.arange(tok_dev, dtype=jnp.int32)
    combine = jnp.where(
        safe_idx.reshape(-1)[None, :] == token_ids[:, None], weight_flat[None, :], 0.0
    )
    mixed = jnp.dot(
        combine, returned.reshape(-1, width).astype(jnp.float32), precision=lax.Precision.HIGHEST
    )
    return mixed.astype(jnp.bfloat16)


def solution(mesh):
    return jax.shard_map(
        per_device,
        mesh=mesh,
        in_specs=(
            P(("dp", "expert"), None),
            P(None, ("dp", "expert")),
            P(None, ("dp", "expert")),
            P("expert", None, "dp"),
            P("expert", None, "dp"),
            P("expert", "dp", None),
        ),
        out_specs=P(("dp", "expert"), None),
        check_vma=False,
    )
```

profile of v0, /device:TPU:0, one launch (start us, length us, event | category | flops | bytes accessed | tf_op | source)
XLA Modules:
  0.0 161.7 jit_solution(17055922872757218782)
XLA Ops:
  6.5 0.0 copy-start
  6.5 0.0 all-gather.2.cloned.1.call-start
  6.5 0.8 broadcast_select_fusion
  7.3 0.7 compare_and_fusion
  8.0 0.1 reshape.81
  8.1 0.0 copy-done
  8.1 0.6 gather_fusion
  8.8 0.1 gather.7
  8.8 0.1 select_select_fusion
  9.0 8.7 %all_to_all.21 = bf16[4,4,4096]{2,1,0:T(4,128)(2,1)S(1)} all-to-all(bf16[4,4,4096]{2,1,0:T(4,128)(2,1)S(1)} %select_select_fusion), channel_id=1, replica_groups=mesh['dp'=8,'expert'=4] {'expert'}, dimensions={0} | all-to-all | bytes 262144 | tf_op jit(solution)/shard_map/all_to_all | solution.py:21
  17.6 0.7 all_to_all.7
  18.3 0.0 all-gather.2.cloned.1.call-update
  18.3 0.0 reduce-scatter.2.cloned.1.call-start
  18.4 40.7 %all-gather.2.cloned.1.call-done = bf16[1,128,4096]{2,1,0:T(8,128)(2,1)} async-done(((bf16[1,16,4096]{2,1,0:T(8,128)(2,1)}), bf16[1,128,4096]{2,1,0:T(8,128)(2,1)}) %all-gather.2.cloned.1.call-update) | async-done | bytes 1048592 | tf_op jit(solution)/shard_map/all_gather | solution.py:23
  59.1 0.0 copy-start.1
  59.1 5.0 %fusion.4 = f32[128,1024]{1,0:T(8,128)S(1)} fusion(bf16[1,4096,1024]{2,1,0:T(8,128)(2,1)} %param.9, bf16[1,128,4096]{2,1,0:T(8,128)(2,1)} %all-gather.2.cloned.1.call-done), kind=kOutput, calls=%fused_computation.5 | convolution fusion | flops 1073741824 | bytes 9961472 | tf_op jit(solution)/shard_map/erd,edf->erf/dot_general | solution.py:8
  64.1 0.0 copy-done.1
  64.1 9.6 %fusion.6 = f32[1,128,4096]{2,1,0:T(8,128)} fusion(bf16[1,1024,4096]{2,1,0:T(8,128)(2,1)} %param.11, bf16[1,4096,1024]{2,1,0:T(8,128)(2,1)} %param.10, bf16[1,128,4096]{2,1,0:T(8,128)(2,1)S(1)} %copy-done.1, f32[128,1024]{1,0:T(8,128)S(1)} %fusion.4), kind=kOutput, calls=%fused_computation.7 | convolution fusion | flops 2148270080 | bytes 20447232 | tf_op jit(solution)/shard_map/erf,efd->erd/dot_general | solution.py:11
  73.7 0.0 reduce-scatter.2.cloned.1.call-update
  73.7 67.3 %reduce-scatter.2.cloned.1.call-done = f32[1,16,4096]{2,1,0:T(8,128)} async-done(((f32[1,128,4096]{2,1,0:T(8,128)}), f32[1,16,4096]{2,1,0:T(8,128)}) %reduce-scatter.2.cloned.1.call-update) | async-done | bytes 262160 | tf_op jit(solution)/shard_map/reduce_scatter | solution.py:25
  141.0 1.0 convert_element_type.14
  142.0 0.2 copy.15
  142.2 0.5 broadcast.57
  142.7 1.4 reduce
  144.1 0.8 reshape.95
  144.9 3.3 %all-to-all-start.1 = ((bf16[4,2,8192]{2,1,0:T(2,128)(2,1)}), bf16[4,2,8192]{2,1,0:T(2,128)(2,1)S(1)}, u32[]{:S(2)}, u32[]{:S(2)}) async-start(bf16[4,2,8192]{2,1,0:T(2,128)(2,1)} %reshape.95), calls=%async_computation.2 | async-start | bytes 262144 | tf_op jit(solution)/shard_map/all_to_all | solution.py:26
  148.2 0.1 eq.15
  148.3 0.1 broadcast_in_dim.45
  148.4 4.4 %all-to-all-done.1 = bf16[4,2,8192]{2,1,0:T(2,128)(2,1)S(1)} async-done(((bf16[4,2,8192]{2,1,0:T(2,128)(2,1)}), bf16[4,2,8192]{2,1,0:T(2,128)(2,1)S(1)}, u32[]{:S(2)}, u32[]{:S(2)}) %all-to-all-start.1) | async-done | bytes 131104 | tf_op jit(solution)/shard_map/all_to_all | solution.py:26
  152.8 0.1 reshape.96
  152.9 2.0 %convolution_convert_fusion = bf16[128,4096]{1,0:T(8,128)(2,1)} fusion(bf16[1,16,4096]{2,0,1:T(2,128)(2,1)S(1)} %bitcast.36, f32[16]{0:T(128)S(1)} %broadcast_in_dim.45, s32[16]{0:T(128)S(1)} %eq.15), kind=kOutput, calls=%fused_computation.8 | convolution fusion | flops 101191680 | bytes 1179776 | tf_op jit(solution)/shard_map/dot_general | solution.py:34
  (2 shorter events, 0.0 us)
Async XLA Ops:
  6.5 1.6 copy-start
  6.5 52.5 %all-gather.2.cloned.1.call-start = ((), (), s32[]{:S(2)}) async-start(), calls=%async_computation.3 | async-start | bytes 1179648 | tf_op jit(solution)/shard_map/all_gather | solution.py:23
  18.3 122.7 %reduce-scatter.2.cloned.1.call-start = ((), (), s32[]{:S(2)}) async-start(), calls=%async_computation.4 | async-start | bytes 2359296 | tf_op jit(solution)/shard_map/reduce_scatter | solution.py:25
  59.1 5.0 %copy-start.1 = (bf16[1,128,4096]{2,1,0:T(8,128)(2,1)S(1)}, bf16[1,128,4096]{2,1,0:T(8,128)(2,1)}, u32[]{:S(2)}) copy-start(bf16[1,128,4096]{2,1,0:T(8,128)(2,1)} %all-gather.2.cloned.1.call-done) | copy-start | bytes 3145732
  144.9 7.9 %all-to-all-start.1 = ((bf16[4,2,8192]{2,1,0:T(2,128)(2,1)}), bf16[4,2,8192]{2,1,0:T(2,128)(2,1)S(1)}, u32[]{:S(2)}, u32[]{:S(2)}) async-start(bf16[4,2,8192]{2,1,0:T(2,128)(2,1)} %reshape.95), calls=%async_computation.2 | async-start | bytes 262144 | tf_op jit(solution)/shard_map/all_to_all | solution.py:26
Sparse Core Ops, SparseCore 0:
  18.5 40.5 all-gather.1
  73.8 67.1 reduce-scatter.1
where the time goes:
time: 162 us
  waiting for transfers between devices  112 us (69%)
  matrix products  16.6 us (10%)
  between operations  13.5 us (8%)
  blocking collectives  8.67 us (5%)
  other arithmetic  3.97 us (2%)
  starting transfers between devices  3.37 us (2%)
  local copies, waits for them, and re-layouts  3.28 us (2%)
    reduce_scatter x1, waiting for transfers between devices, per_device(): lax.psum_scatter(partial_value, 'dp', scatter_dimension=1, tiled=True)  67.3 us
    all_gather x1, waiting for transfers between devices, per_device(): lax.all_gather(arrived, 'dp', axis=1, tiled=True)  40.7 us
    dot_general x1, matrix products, expert_ffn(): jnp.einsum('erf,efd->erd', hidden, w_down, preferred_element_type=jnp.flo...  9.57 us
    all_to_all x1, blocking collectives, per_device(): lax.all_to_all(sel_rows, 'expert', split_axis=0, concat_axis=1, tiled=True)  8.67 us
    dot_general x1, matrix products, expert_ffn(): jnp.einsum('erd,edf->erf', block_rows, w_gate, preferred_element_type=jnp...  5.03 us
    all_to_all x1, waiting for transfers between devices, per_device(): lax.all_to_all(summed.astype(jnp.bfloat16), 'expert', split_axis=1, conca...  4.4 us
    all_to_all x1, starting transfers between devices, per_device(): lax.all_to_all(summed.astype(jnp.bfloat16), 'expert', split_axis=1, conca...  3.33 us
  transfers between devices with their start and end apart: 3, of which 3 were waited for; matrix products, arithmetic and copies ran while one was open for 0% of the time, Pallas kernels for 0%

commit v1 on v0

--- a/solution.py
+++ b/solution.py
@@ -18,7 +18,12 @@
     safe_idx = jnp.where(is_live, select, 0)
     sel_rows = jnp.take(tokens, safe_idx.reshape(-1), axis=0).reshape(experts, slot_count, width)
     sel_rows = jnp.where(is_live[:, :, None], sel_rows, 0)
-    arrived = lax.all_to_all(sel_rows, "expert", split_axis=0, concat_axis=1, tiled=True)
+    arrived = jnp.concatenate(
+        lax.all_to_all(
+            jnp.stack(jnp.split(sel_rows, lax.axis_size("expert"), axis=0)), "expert", 0, 0
+        ),
+        axis=1,
+    )
     partial_value = expert_ffn(
         lax.all_gather(arrived, "dp", axis=1, tiled=True), w_gate, w_up, w_down
     )

time: 162 us -> 162 us (level)
  no operation moved by 1% of the time
where the time goes in v1:
time: 162 us
  waiting for transfers between devices  112 us (69%)
  matrix products  16.6 us (10%)
  between operations  13.5 us (8%)
  blocking collectives  8.67 us (5%)
  other arithmetic  4.09 us (3%)
  starting transfers between devices  3.37 us (2%)
  local copies, waits for them, and re-layouts  3.33 us (2%)
    reduce_scatter x1, waiting for transfers between devices, per_device(): lax.psum_scatter(partial_value, 'dp', scatter_dimension=1, tiled=True)  67.3 us
    all_gather x1, waiting for transfers between devices, per_device(): lax.all_gather(arrived, 'dp', axis=1, tiled=True)  40.7 us
    dot_general x1, matrix products, expert_ffn(): jnp.einsum('erf,efd->erd', hidden, w_down, preferred_element_type=jnp.flo...  9.57 us
    all_to_all x1, blocking collectives, per_device(): lax.all_to_all(jnp.stack(jnp.split(sel_rows, lax.axis_size('expert'), axi...  8.67 us
    dot_general x1, matrix products, expert_ffn(): jnp.einsum('erd,edf->erf', block_rows, w_gate, preferred_element_type=jnp...  5.04 us
    all_to_all x1, waiting for transfers between devices, per_device(): lax.all_to_all(summed.astype(jnp.bfloat16), 'expert', split_axis=1, conca...  4.4 us
    all_to_all x1, starting transfers between devices, per_device(): lax.all_to_all(summed.astype(jnp.bfloat16), 'expert', split_axis=1, conca...  3.33 us
  transfers between devices with their start and end apart: 3, of which 3 were waited for; matrix products, arithmetic and copies ran while one was open for 0% of the time, Pallas kernels for 0%

profile of v1, /device:TPU:0, one launch (start us, length us, event | category | flops | bytes accessed | tf_op | source)
XLA Modules:
  0.0 162.0 jit_solution(2293305821855917495)
XLA Ops:
  6.5 0.0 copy-start
  6.5 0.0 all-gather.2.cloned.1.call-start
  6.5 0.8 broadcast_select_fusion
  7.3 0.7 compare_and_fusion
  8.0 0.1 reshape.81
  8.1 0.0 copy-done
  8.1 0.6 gather_fusion
  8.8 0.1 gather.7
  8.8 0.1 select_select_fusion
  9.0 0.1 pad_maximum_fusion
  9.1 8.7 %all_to_all.14 = bf16[4,1,4,4096]{3,2,1,0:T(4,128)(2,1)S(1)} all-to-all(bf16[4,1,4,4096]{3,2,1,0:T(4,128)(2,1)S(1)} %pad_maximum_fusion), channel_id=1, replica_groups=mesh['dp'=8,'expert'=4] {'expert'}, dimensions={0} | all-to-all | bytes 262144 | tf_op jit(solution)/shard_map/all_to_all | solution.py:22
  17.8 0.7 reshape.82
  18.5 0.0 all-gather.2.cloned.1.call-update
  18.5 0.0 reduce-scatter.2.cloned.1.call-start
  18.6 40.7 %all-gather.2.cloned.1.call-done = bf16[1,128,4096]{2,1,0:T(8,128)(2,1)} async-done(((bf16[1,16,4096]{2,1,0:T(8,128)(2,1)}), bf16[1,128,4096]{2,1,0:T(8,128)(2,1)}) %all-gather.2.cloned.1.call-update) | async-done | bytes 1048592 | tf_op jit(solution)/shard_map/all_gather | solution.py:28
  59.2 0.0 copy-start.1
  59.2 5.0 %fusion.4 = f32[128,1024]{1,0:T(8,128)S(1)} fusion(bf16[1,4096,1024]{2,1,0:T(8,128)(2,1)} %param.9, bf16[1,128,4096]{2,1,0:T(8,128)(2,1)} %all-gather.2.cloned.1.call-done), kind=kOutput, calls=%fused_computation.5 | convolution fusion | flops 1073741824 | bytes 9961472 | tf_op jit(solution)/shard_map/erd,edf->erf/dot_general | solution.py:8
  64.3 0.0 copy-done.1
  64.3 9.6 %fusion.6 = f32[1,128,4096]{2,1,0:T(8,128)} fusion(bf16[1,1024,4096]{2,1,0:T(8,128)(2,1)} %param.11, bf16[1,4096,1024]{2,1,0:T(8,128)(2,1)} %param.10, bf16[1,128,4096]{2,1,0:T(8,128)(2,1)S(1)} %copy-done.1, f32[128,1024]{1,0:T(8,128)S(1)} %fusion.4), kind=kOutput, calls=%fused_computation.7 | convolution fusion | flops 2148270080 | bytes 20447232 | tf_op jit(solution)/shard_map/erf,efd->erd/dot_general | solution.py:11
  73.9 0.0 reduce-scatter.2.cloned.1.call-update
  73.9 67.3 %reduce-scatter.2.cloned.1.call-done = f32[1,16,4096]{2,1,0:T(8,128)} async-done(((f32[1,128,4096]{2,1,0:T(8,128)}), f32[1,16,4096]{2,1,0:T(8,128)}) %reduce-scatter.2.cloned.1.call-update) | async-done | bytes 262160 | tf_op jit(solution)/shard_map/reduce_scatter | solution.py:30
  141.2 1.0 convert_element_type.14
  142.2 0.2 copy.15
  142.5 0.5 broadcast.57
  143.0 1.4 reduce
  144.3 0.8 reshape.96
  145.1 3.3 %all-to-all-start.1 = ((bf16[4,2,8192]{2,1,0:T(2,128)(2,1)}), bf16[4,2,8192]{2,1,0:T(2,128)(2,1)S(1)}, u32[]{:S(2)}, u32[]{:S(2)}) async-start(bf16[4,2,8192]{2,1,0:T(2,128)(2,1)} %reshape.96), calls=%async_computation.2 | async-start | bytes 262144 | tf_op jit(solution)/shard_map/all_to_all | solution.py:31
  148.5 0.1 eq.15
  148.5 0.1 broadcast_in_dim.45
  148.6 4.4 %all-to-all-done.1 = bf16[4,2,8192]{2,1,0:T(2,128)(2,1)S(1)} async-done(((bf16[4,2,8192]{2,1,0:T(2,128)(2,1)}), bf16[4,2,8192]{2,1,0:T(2,128)(2,1)S(1)}, u32[]{:S(2)}, u32[]{:S(2)}) %all-to-all-start.1) | async-done | bytes 131104 | tf_op jit(solution)/shard_map/all_to_all | solution.py:31
  153.0 0.1 reshape.97
  153.1 2.0 %convolution_convert_fusion = bf16[128,4096]{1,0:T(8,128)(2,1)} fusion(bf16[1,16,4096]{2,0,1:T(2,128)(2,1)S(1)} %bitcast.44, f32[16]{0:T(128)S(1)} %broadcast_in_dim.45, s32[16]{0:T(128)S(1)} %eq.15), kind=kOutput, calls=%fused_computation.8 | convolution fusion | flops 101191680 | bytes 1179776 | tf_op jit(solution)/shard_map/dot_general | solution.py:39
  (3 shorter events, 0.1 us)
Async XLA Ops:
  6.5 1.6 copy-start
  6.5 52.7 %all-gather.2.cloned.1.call-start = ((), (), s32[]{:S(2)}) async-start(), calls=%async_computation.3 | async-start | bytes 1179648 | tf_op jit(solution)/shard_map/all_gather | solution.py:28
  18.5 122.7 %reduce-scatter.2.cloned.1.call-start = ((), (), s32[]{:S(2)}) async-start(), calls=%async_computation.4 | async-start | bytes 2359296 | tf_op jit(solution)/shard_map/reduce_scatter | solution.py:30
  59.2 5.0 %copy-start.1 = (bf16[1,128,4096]{2,1,0:T(8,128)(2,1)S(1)}, bf16[1,128,4096]{2,1,0:T(8,128)(2,1)}, u32[]{:S(2)}) copy-start(bf16[1,128,4096]{2,1,0:T(8,128)(2,1)} %all-gather.2.cloned.1.call-done) | copy-start | bytes 3145732
  145.1 7.9 %all-to-all-start.1 = ((bf16[4,2,8192]{2,1,0:T(2,128)(2,1)}), bf16[4,2,8192]{2,1,0:T(2,128)(2,1)S(1)}, u32[]{:S(2)}, u32[]{:S(2)}) async-start(bf16[4,2,8192]{2,1,0:T(2,128)(2,1)} %reshape.96), calls=%async_computation.2 | async-start | bytes 262144 | tf_op jit(solution)/shard_map/all_to_all | solution.py:31
Sparse Core Ops, SparseCore 0:
  18.6 40.5 all-gather.1
  74.0 67.1 reduce-scatter.1
